TPU v7x, 128 devices: a whole 4x4x4 slice. The times are simulated.
128 devices in a mesh: batch: 32 (over z, y_hi, x), head: 4 (over y_lo, core).
Axes of the slice: x: 4, y: 4 (y_hi: 2, y_lo: 2; y = y_hi * 2 + y_lo), z: 4, core: 2. Of those that a mesh axis runs over, the one named last changes fastest.
Arguments:
- features: bfloat16 [4096, 24, 512], P(('batch', 'head')), may hold values from -6 to 6
- state_h: bfloat16 [4096, 1024], P(('batch', 'head')), may hold values from -0.8984375 to 0.8984375
- state_c: bfloat16 [4096, 1024], P(('batch', 'head')), may hold values from -4 to 4
- valid: int32 [4096], P(('batch', 'head')), may hold values 0 or 1
- ends: int32 [4096, 24], P(('batch', 'head')), may hold values 0 or 1
- policy: int32 [4096, 1], P(('batch', 'head')), may hold values from 0 to 31; in each aligned block of 32 rows (0 to 31, 32 to 63, ...) at most 2 rows name the same one
- actions: int32 [4096, 16], P(('batch', 'head')), may hold values from 0 to 17
- w_input: bfloat16 [512, 4, 1024], P('batch', None, 'head'), may hold values from -0.25 to 0.25
- w_recur: bfloat16 [1024, 4, 1024], P('batch', None, 'head'), may hold values from -0.1875 to 0.1875
- lstm_bias: float32 [4, 1024], replicated, may hold values from -3 to 5
- w_hidden: bfloat16 [32, 1024, 1024], P('head'), may hold values from -0.1875 to 0.1875
- w_value: bfloat16 [32, 512], P('head'), may hold values from -0.25 to 0.25
- w_advantage: bfloat16 [32, 512, 18], P('head'), may hold values from -0.25 to 0.25
Outputs:
- q_values: float32 [4096, 16, 18], P(('batch', 'head'))
- q_taken: float32 [4096, 16], P(('batch', 'head'))
Inputs may be any that keep to these rules, and one draw needn't show every extreme that they name: In the rows of one device no policy appears more than 2 times, and some policy appears exactly 2 times.
All inputs are finite; a program needn't handle non-finite values. No bound on the sum of `valid` or of `ends` on one device may be relied on, other than what follows from the above.
Results may differ from a plain program's by a relative error of at most 0.007.
Values may be sent and summed in bfloat16 or wider, within the bound.
A program may use at most 128 MiB of HBM per device.

v0:
```python
import jax
import jax.numpy as jnp
from jax import lax
from jax.sharding import PartitionSpec as P

ACTIONS = 18
POLICIES = 32
CAPP = 2


def in_one_piece(arrays, axis, dim, along):
    widths = [a.shape[along] for a in arrays]
    both = jnp.concatenate(arrays, axis=along)
    filled = lax.all_gather(both, axis, axis=dim, tiled=True)
    return tuple(jnp.split(filled, [sum(widths[:k]) for k in range(1, len(widths))], axis=along))


def slot_table(owners, per_source, capacity, policies):
    count = owners.shape[0]
    sources = count // per_source
    place = jnp.arange(count, dtype=jnp.int32)
    anchor = place // per_source
    before = (
        (owners[:, None] == owners[None, :])
        & (anchor[:, None] == anchor[None, :])
        & (place[None, :] < place[:, None])
    )
    rank = jnp.sum(before.astype(jnp.int32), axis=1)
    target = owners * (sources * capacity) + anchor * capacity + rank
    total = policies * sources * capacity
    return (jnp.arange(total, dtype=jnp.int32)[:, None] == target[None, :]).astype(jnp.bfloat16)


def lstm_cell(pre_t, full_h, cell_state, keep_t, w_flat, bias, width):
    full_h = full_h * keep_t[:, None].astype(jnp.bfloat16)
    cell_state = cell_state * keep_t[:, None]
    gates = (
        pre_t
        + jnp.dot(full_h, w_flat, preferred_element_type=jnp.float32).reshape(-1, 4, width)
        + bias
    )
    cell_state = jax.nn.sigmoid(gates[:, 1]) * cell_state + jax.nn.sigmoid(gates[:, 0]) * jnp.tanh(
        gates[:, 2]
    )
    new_h = (jax.nn.sigmoid(gates[:, 3]) * jnp.tanh(cell_state)).astype(jnp.bfloat16)
    return (new_h, cell_state)


def shards(
    features,
    state_h,
    state_c,
    valid,
    ends,
    policy,
    actions,
    w_input,
    w_recur,
    lstm_bias,
    w_hidden,
    w_value,
    w_advantage,
):
    seq_dev, steps, width_e = features.shape
    width_h = state_h.shape[1]
    learn = actions.shape[1]
    burn = steps - learn
    keep_start = valid.astype(jnp.bfloat16)[:, None]
    start_h = state_h * keep_start
    start_c = state_c * keep_start
    w_in_rows, w_rec_rows = in_one_piece((w_input, w_recur), "head", 2, 0)
    feat_flat = features.transpose(1, 0, 2).reshape(-1, width_e)
    w_in_full = lax.all_gather(w_in_rows, "batch", axis=0, tiled=True).reshape(width_e, 4 * width_h)
    pre = jnp.dot(feat_flat, w_in_full, preferred_element_type=jnp.float32).reshape(
        steps, seq_dev, 4, width_h
    )
    w_flat = lax.all_gather(w_rec_rows, "batch", axis=0, tiled=True).reshape(width_h, 4 * width_h)
    keeps = 1.0 - ends.astype(jnp.float32).T

    def advance(carry, inputs):
        full_h, cell_state = carry
        pre_t, keep_t = inputs
        new_h, cell_state = lstm_cell(pre_t, full_h, cell_state, keep_t, w_flat, lstm_bias, width_h)
        return ((new_h, cell_state), new_h)

    _, outputs = lax.scan(advance, (start_h, start_c.astype(jnp.float32)), (pre, keeps))
    learned = outputs[burn:]
    table = slot_table(policy[:, 0], seq_dev, CAPP, POLICIES)
    packed = jnp.einsum("ks,tsu->ktu", table, learned, preferred_element_type=jnp.float32).astype(
        jnp.bfloat16
    )
    packed = packed.reshape(POLICIES, CAPP, learn, width_h)
    routed = lax.all_to_all(packed, "head", split_axis=0, concat_axis=1, tiled=True)
    local_heads, slots = (routed.shape[0], routed.shape[1])
    rows = routed.reshape(local_heads, slots * learn, width_h)
    mid = jnp.einsum("prh,phk->prk", rows, w_hidden, preferred_element_type=jnp.float32)
    mid = jnp.maximum(mid, 0.0).astype(jnp.bfloat16)
    branch = w_value.shape[1]
    value = jnp.einsum(
        "prk,pk->pr", mid[:, :, :branch], w_value, preferred_element_type=jnp.float32
    )
    advantage = jnp.einsum(
        "prk,pka->pra", mid[:, :, branch:], w_advantage, preferred_element_type=jnp.float32
    )
    q_local = value[:, :, None] + advantage - jnp.mean(advantage, axis=-1, keepdims=True)
    q_local = q_local.reshape(local_heads, slots, learn, ACTIONS)
    returned = lax.all_to_all(
        q_local.astype(jnp.bfloat16), "head", split_axis=1, concat_axis=0, tiled=True
    ).astype(q_local.dtype)
    own_table = slot_table(policy[:, 0], seq_dev, CAPP, POLICIES).astype(jnp.float32)
    q_values = jnp.dot(
        own_table.T,
        returned.reshape(POLICIES * CAPP, learn * ACTIONS),
        precision=lax.Precision.HIGHEST,
    ).reshape(seq_dev, learn, ACTIONS)
    chosen = actions[:, :, None] == jnp.arange(ACTIONS, dtype=jnp.int32)[None, None, :]
    q_taken = jnp.sum(jnp.where(chosen, q_values, 0.0), axis=-1)
    return (q_values, q_taken)


def solution(mesh):
    return jax.shard_map(
        shards,
        mesh=mesh,
        in_specs=(
            P(("batch", "head"), None, None),
            P(("batch", "head"), None),
            P(("batch", "head"), None),
            P(("batch", "head")),
            P(("batch", "head"), None),
            P(("batch", "head"), None),
            P(("batch", "head"), None),
            P("batch", None, "head"),
            P("batch", None, "head"),
            P(),
            P("head", None, None),
            P("head", None),
            P("head", None, None),
        ),
        out_specs=(P(("batch", "head"), None, None), P(("batch", "head"), None)),
        check_vma=False,
    )
```

profile of v0, /device:TPU:1, one launch (start us, length us, event | category | flops | bytes accessed | tf_op | source)
XLA Modules:
  0.0 450.7 jit_solution(334485971511818191)
XLA Ops:
  7.3 1.0 pad_maximum_fusion
  8.3 7.9 %all_gather.9 = bf16[48,4,1024]{2,1,0:T(4,128)(2,1)S(1)} all-gather(bf16[48,4,256]{2,1,0:T(4,128)(2,1)S(1)} %pad_maximum_fusion), channel_id=1, replica_groups=mesh['batch'=32,'head'=4] {'head'}, dimensions={2}, use_global_device_ids=true | all-gather | bytes 491520 | tf_op jit(solution)/shard_map/all_gather | solution.py:14
  18.4 79.2 %all-gather.3.cloned.1.call-done = bf16[512,4,1024]{2,1,0:T(4,128)(2,1)} async-done(((bf16[16,4,1024]{2,1,0:T(4,128)(2,1)}), bf16[512,4,1024]{2,1,0:T(4,128)(2,1)}) %all-gather.3.cloned.1.call-update) | async-done | bytes 4194320 | tf_op jit(solution)/shard_map/all_gather | solution.py:73
  97.6 4.5 copy.61
  102.1 6.6 %convolution_bitcast_fusion = f32[768,4096]{0,1:T(8,128)} fusion(bf16[512,4096]{1,0:T(8,128)(2,1)S(1)} %bitcast.92, bf16[768,512]{1,0:T(8,128)(2,1)S(1)} %bitcast.96), kind=kOutput, calls=%fused_computation.30 | convolution fusion | flops 3221225472 | bytes 17563648 | tf_op jit(solution)/shard_map/dot_general | solution.py:74
  108.7 12.7 %copy.47 = f32[768,4096]{1,0:T(8,128)} copy(f32[768,4096]{0,1:T(8,128)} %convolution_bitcast_fusion) | data formatting | bytes 25165824 | tf_op jit(solution)/shard_map/dot_general | solution.py:74
  121.3 15.6 %reshape.110 = f32[24,32,4,1024]{3,2,1,0:T(4,128)} reshape(f32[768,4096]{1,0:T(8,128)} %copy.47) | data formatting | bytes 25165824 | tf_op jit(solution)/shard_map/reshape | solution.py:74
  137.0 65.1 %all-gather.5.cloned.1.call-done = bf16[1024,4,1024]{2,1,0:T(4,128)(2,1)} async-done(((bf16[32,4,1024]{2,1,0:T(4,128)(2,1)}), bf16[1024,4,1024]{2,1,0:T(4,128)(2,1)}) %all-gather.5.cloned.1.call-update) | async-done | bytes 8388624 | tf_op jit(solution)/shard_map/all_gather | solution.py:77
  202.1 12.1 %copy.62 = bf16[128,8,4,1024]{3,1,2,0:T(8,128)(2,1)} copy(bf16[128,8,4,1024]{3,2,1,0:T(4,128)(2,1)} %bitcast.89) | data formatting | bytes 16777216
  214.2 173.0 %while.14 = (s32[]{:T(128)}, bf16[32,1024]{1,0:T(8,128)(2,1)S(1)}, f32[32,1024]{1,0:T(8,128)S(1)}, bf16[24,32,1024]{2,1,0:T(8,128)(2,1)}, f32[24,32,4,1024]{3,2,...) while((s32[]{:T(128)}, bf16[32,1024]{1,0:T(8,128)(2,1)S(1)}, ...), condition=%wide.region_2.3_spmd, body=%wide.region_1.2_spmd.sunk | while | flops 269221920 | bytes 12534885 | solution.py:86
  214.2 5.0 %fusion.55 = f32[32,4096]{1,0:T(8,128)S(1)} fusion(bf16[1024,4096]{1,0:T(8,128)(2,1)} %get-tuple-element.171, bf16[32,1024]{1,0:T(8,128)(2,1)S(1)} %get-tuple-element.157, bf16[32]{0:T(256)(128)(2,1)S(1)} %get-tuple-element.142), kind=kOutput, calls=%fused_computation.24.clone.1 | convolution fusion | flops 268468224 | bytes 8978496 | tf_op jit(solution)/shard_map/while/body/eval_jaxpr/dot_general | solution.py:39
  219.2 1.1 constant_dynamic-slice_fusion.3
  221.4 5.0 %fusion.55 = f32[32,4096]{1,0:T(8,128)S(1)} fusion(bf16[1024,4096]{1,0:T(8,128)(2,1)} %get-tuple-element.171, bf16[32,1024]{1,0:T(8,128)(2,1)S(1)} %get-tuple-element.157, bf16[32]{0:T(256)(128)(2,1)S(1)} %get-tuple-element.142), kind=kOutput, calls=%fused_computation.24.clone.1 | convolution fusion | flops 268468224 | bytes 8978496 | tf_op jit(solution)/shard_map/while/body/eval_jaxpr/dot_general | solution.py:39
  226.4 1.1 constant_dynamic-slice_fusion.3
  228.6 5.0 %fusion.55 = f32[32,4096]{1,0:T(8,128)S(1)} fusion(bf16[1024,4096]{1,0:T(8,128)(2,1)} %get-tuple-element.171, bf16[32,1024]{1,0:T(8,128)(2,1)S(1)} %get-tuple-element.157, bf16[32]{0:T(256)(128)(2,1)S(1)} %get-tuple-element.142), kind=kOutput, calls=%fused_computation.24.clone.1 | convolution fusion | flops 268468224 | bytes 8978496 | tf_op jit(solution)/shard_map/while/body/eval_jaxpr/dot_general | solution.py:39
  233.6 1.1 constant_dynamic-slice_fusion.3
  235.8 5.0 %fusion.55 = f32[32,4096]{1,0:T(8,128)S(1)} fusion(bf16[1024,4096]{1,0:T(8,128)(2,1)} %get-tuple-element.171, bf16[32,1024]{1,0:T(8,128)(2,1)S(1)} %get-tuple-element.157, bf16[32]{0:T(256)(128)(2,1)S(1)} %get-tuple-element.142), kind=kOutput, calls=%fused_computation.24.clone.1 | convolution fusion | flops 268468224 | bytes 8978496 | tf_op jit(solution)/shard_map/while/body/eval_jaxpr/dot_general | solution.py:39
  240.8 1.1 constant_dynamic-slice_fusion.3
  243.0 5.0 %fusion.55 = f32[32,4096]{1,0:T(8,128)S(1)} fusion(bf16[1024,4096]{1,0:T(8,128)(2,1)} %get-tuple-element.171, bf16[32,1024]{1,0:T(8,128)(2,1)S(1)} %get-tuple-element.157, bf16[32]{0:T(256)(128)(2,1)S(1)} %get-tuple-element.142), kind=kOutput, calls=%fused_computation.24.clone.1 | convolution fusion | flops 268468224 | bytes 8978496 | tf_op jit(solution)/shard_map/while/body/eval_jaxpr/dot_general | solution.py:39
  248.0 1.1 constant_dynamic-slice_fusion.3
  250.2 5.0 %fusion.55 = f32[32,4096]{1,0:T(8,128)S(1)} fusion(bf16[1024,4096]{1,0:T(8,128)(2,1)} %get-tuple-element.171, bf16[32,1024]{1,0:T(8,128)(2,1)S(1)} %get-tuple-element.157, bf16[32]{0:T(256)(128)(2,1)S(1)} %get-tuple-element.142), kind=kOutput, calls=%fused_computation.24.clone.1 | convolution fusion | flops 268468224 | bytes 8978496 | tf_op jit(solution)/shard_map/while/body/eval_jaxpr/dot_general | solution.py:39
  255.2 1.1 constant_dynamic-slice_fusion.3
  257.4 5.0 %fusion.55 = f32[32,4096]{1,0:T(8,128)S(1)} fusion(bf16[1024,4096]{1,0:T(8,128)(2,1)} %get-tuple-element.171, bf16[32,1024]{1,0:T(8,128)(2,1)S(1)} %get-tuple-element.157, bf16[32]{0:T(256)(128)(2,1)S(1)} %get-tuple-element.142), kind=kOutput, calls=%fused_computation.24.clone.1 | convolution fusion | flops 268468224 | bytes 8978496 | tf_op jit(solution)/shard_map/while/body/eval_jaxpr/dot_general | solution.py:39
  262.4 1.1 constant_dynamic-slice_fusion.3
  264.6 5.0 %fusion.55 = f32[32,4096]{1,0:T(8,128)S(1)} fusion(bf16[1024,4096]{1,0:T(8,128)(2,1)} %get-tuple-element.171, bf16[32,1024]{1,0:T(8,128)(2,1)S(1)} %get-tuple-element.157, bf16[32]{0:T(256)(128)(2,1)S(1)} %get-tuple-element.142), kind=kOutput, calls=%fused_computation.24.clone.1 | convolution fusion | flops 268468224 | bytes 8978496 | tf_op jit(solution)/shard_map/while/body/eval_jaxpr/dot_general | solution.py:39
  269.6 1.1 constant_dynamic-slice_fusion.3
  271.9 5.0 %fusion.55 = f32[32,4096]{1,0:T(8,128)S(1)} fusion(bf16[1024,4096]{1,0:T(8,128)(2,1)} %get-tuple-element.171, bf16[32,1024]{1,0:T(8,128)(2,1)S(1)} %get-tuple-element.157, bf16[32]{0:T(256)(128)(2,1)S(1)} %get-tuple-element.142), kind=kOutput, calls=%fused_computation.24.clone.1 | convolution fusion | flops 268468224 | bytes 8978496 | tf_op jit(solution)/shard_map/while/body/eval_jaxpr/dot_general | solution.py:39
  276.8 1.1 constant_dynamic-slice_fusion.3
  279.1 5.0 %fusion.55 = f32[32,4096]{1,0:T(8,128)S(1)} fusion(bf16[1024,4096]{1,0:T(8,128)(2,1)} %get-tuple-element.171, bf16[32,1024]{1,0:T(8,128)(2,1)S(1)} %get-tuple-element.157, bf16[32]{0:T(256)(128)(2,1)S(1)} %get-tuple-element.142), kind=kOutput, calls=%fused_computation.24.clone.1 | convolution fusion | flops 268468224 | bytes 8978496 | tf_op jit(solution)/shard_map/while/body/eval_jaxpr/dot_general | solution.py:39
  284.0 1.1 constant_dynamic-slice_fusion.3
  286.3 5.0 %fusion.55 = f32[32,4096]{1,0:T(8,128)S(1)} fusion(bf16[1024,4096]{1,0:T(8,128)(2,1)} %get-tuple-element.171, bf16[32,1024]{1,0:T(8,128)(2,1)S(1)} %get-tuple-element.157, bf16[32]{0:T(256)(128)(2,1)S(1)} %get-tuple-element.142), kind=kOutput, calls=%fused_computation.24.clone.1 | convolution fusion | flops 268468224 | bytes 8978496 | tf_op jit(solution)/shard_map/while/body/eval_jaxpr/dot_general | solution.py:39
  291.2 1.1 constant_dynamic-slice_fusion.3
  293.5 5.0 %fusion.55 = f32[32,4096]{1,0:T(8,128)S(1)} fusion(bf16[1024,4096]{1,0:T(8,128)(2,1)} %get-tuple-element.171, bf16[32,1024]{1,0:T(8,128)(2,1)S(1)} %get-tuple-element.157, bf16[32]{0:T(256)(128)(2,1)S(1)} %get-tuple-element.142), kind=kOutput, calls=%fused_computation.24.clone.1 | convolution fusion | flops 268468224 | bytes 8978496 | tf_op jit(solution)/shard_map/while/body/eval_jaxpr/dot_general | solution.py:39
  298.5 1.1 constant_dynamic-slice_fusion.3
  300.7 5.0 %fusion.55 = f32[32,4096]{1,0:T(8,128)S(1)} fusion(bf16[1024,4096]{1,0:T(8,128)(2,1)} %get-tuple-element.171, bf16[32,1024]{1,0:T(8,128)(2,1)S(1)} %get-tuple-element.157, bf16[32]{0:T(256)(128)(2,1)S(1)} %get-tuple-element.142), kind=kOutput, calls=%fused_computation.24.clone.1 | convolution fusion | flops 268468224 | bytes 8978496 | tf_op jit(solution)/shard_map/while/body/eval_jaxpr/dot_general | solution.py:39
  305.7 1.1 constant_dynamic-slice_fusion.3
  307.9 5.0 %fusion.55 = f32[32,4096]{1,0:T(8,128)S(1)} fusion(bf16[1024,4096]{1,0:T(8,128)(2,1)} %get-tuple-element.171, bf16[32,1024]{1,0:T(8,128)(2,1)S(1)} %get-tuple-element.157, bf16[32]{0:T(256)(128)(2,1)S(1)} %get-tuple-element.142), kind=kOutput, calls=%fused_computation.24.clone.1 | convolution fusion | flops 268468224 | bytes 8978496 | tf_op jit(solution)/shard_map/while/body/eval_jaxpr/dot_general | solution.py:39
  312.9 1.1 constant_dynamic-slice_fusion.3
  315.1 5.0 %fusion.55 = f32[32,4096]{1,0:T(8,128)S(1)} fusion(bf16[1024,4096]{1,0:T(8,128)(2,1)} %get-tuple-element.171, bf16[32,1024]{1,0:T(8,128)(2,1)S(1)} %get-tuple-element.157, bf16[32]{0:T(256)(128)(2,1)S(1)} %get-tuple-element.142), kind=kOutput, calls=%fused_computation.24.clone.1 | convolution fusion | flops 268468224 | bytes 8978496 | tf_op jit(solution)/shard_map/while/body/eval_jaxpr/dot_general | solution.py:39
  320.1 1.1 constant_dynamic-slice_fusion.3
  322.3 5.0 %fusion.55 = f32[32,4096]{1,0:T(8,128)S(1)} fusion(bf16[1024,4096]{1,0:T(8,128)(2,1)} %get-tuple-element.171, bf16[32,1024]{1,0:T(8,128)(2,1)S(1)} %get-tuple-element.157, bf16[32]{0:T(256)(128)(2,1)S(1)} %get-tuple-element.142), kind=kOutput, calls=%fused_computation.24.clone.1 | convolution fusion | flops 268468224 | bytes 8978496 | tf_op jit(solution)/shard_map/while/body/eval_jaxpr/dot_general | solution.py:39
  327.3 1.1 constant_dynamic-slice_fusion.3
  329.5 5.0 %fusion.55 = f32[32,4096]{1,0:T(8,128)S(1)} fusion(bf16[1024,4096]{1,0:T(8,128)(2,1)} %get-tuple-element.171, bf16[32,1024]{1,0:T(8,128)(2,1)S(1)} %get-tuple-element.157, bf16[32]{0:T(256)(128)(2,1)S(1)} %get-tuple-element.142), kind=kOutput, calls=%fused_computation.24.clone.1 | convolution fusion | flops 268468224 | bytes 8978496 | tf_op jit(solution)/shard_map/while/body/eval_jaxpr/dot_general | solution.py:39
  334.5 1.1 constant_dynamic-slice_fusion.3
  336.7 5.0 %fusion.55 = f32[32,4096]{1,0:T(8,128)S(1)} fusion(bf16[1024,4096]{1,0:T(8,128)(2,1)} %get-tuple-element.171, bf16[32,1024]{1,0:T(8,128)(2,1)S(1)} %get-tuple-element.157, bf16[32]{0:T(256)(128)(2,1)S(1)} %get-tuple-element.142), kind=kOutput, calls=%fused_computation.24.clone.1 | convolution fusion | flops 268468224 | bytes 8978496 | tf_op jit(solution)/shard_map/while/body/eval_jaxpr/dot_general | solution.py:39
  341.7 1.1 constant_dynamic-slice_fusion.3
  344.0 5.0 %fusion.55 = f32[32,4096]{1,0:T(8,128)S(1)} fusion(bf16[1024,4096]{1,0:T(8,128)(2,1)} %get-tuple-element.171, bf16[32,1024]{1,0:T(8,128)(2,1)S(1)} %get-tuple-element.157, bf16[32]{0:T(256)(128)(2,1)S(1)} %get-tuple-element.142), kind=kOutput, calls=%fused_computation.24.clone.1 | convolution fusion | flops 268468224 | bytes 8978496 | tf_op jit(solution)/shard_map/while/body/eval_jaxpr/dot_general | solution.py:39
  348.9 1.1 constant_dynamic-slice_fusion.3
  351.2 5.0 %fusion.55 = f32[32,4096]{1,0:T(8,128)S(1)} fusion(bf16[1024,4096]{1,0:T(8,128)(2,1)} %get-tuple-element.171, bf16[32,1024]{1,0:T(8,128)(2,1)S(1)} %get-tuple-element.157, bf16[32]{0:T(256)(128)(2,1)S(1)} %get-tuple-element.142), kind=kOutput, calls=%fused_computation.24.clone.1 | convolution fusion | flops 268468224 | bytes 8978496 | tf_op jit(solution)/shard_map/while/body/eval_jaxpr/dot_general | solution.py:39
  356.1 1.1 constant_dynamic-slice_fusion.3
  358.4 5.0 %fusion.55 = f32[32,4096]{1,0:T(8,128)S(1)} fusion(bf16[1024,4096]{1,0:T(8,128)(2,1)} %get-tuple-element.171, bf16[32,1024]{1,0:T(8,128)(2,1)S(1)} %get-tuple-element.157, bf16[32]{0:T(256)(128)(2,1)S(1)} %get-tuple-element.142), kind=kOutput, calls=%fused_computation.24.clone.1 | convolution fusion | flops 268468224 | bytes 8978496 | tf_op jit(solution)/shard_map/while/body/eval_jaxpr/dot_general | solution.py:39
  363.3 1.1 constant_dynamic-slice_fusion.3
  365.6 5.0 %fusion.55 = f32[32,4096]{1,0:T(8,128)S(1)} fusion(bf16[1024,4096]{1,0:T(8,128)(2,1)} %get-tuple-element.171, bf16[32,1024]{1,0:T(8,128)(2,1)S(1)} %get-tuple-element.157, bf16[32]{0:T(256)(128)(2,1)S(1)} %get-tuple-element.142), kind=kOutput, calls=%fused_computation.24.clone.1 | convolution fusion | flops 268468224 | bytes 8978496 | tf_op jit(solution)/shard_map/while/body/eval_jaxpr/dot_general | solution.py:39
  370.5 1.1 constant_dynamic-slice_fusion.3
  372.8 5.0 %fusion.55 = f32[32,4096]{1,0:T(8,128)S(1)} fusion(bf16[1024,4096]{1,0:T(8,128)(2,1)} %get-tuple-element.171, bf16[32,1024]{1,0:T(8,128)(2,1)S(1)} %get-tuple-element.157, bf16[32]{0:T(256)(128)(2,1)S(1)} %get-tuple-element.142), kind=kOutput, calls=%fused_computation.24.clone.1 | convolution fusion | flops 268468224 | bytes 8978496 | tf_op jit(solution)/shard_map/while/body/eval_jaxpr/dot_general | solution.py:39
  377.8 1.1 constant_dynamic-slice_fusion.3
  380.0 5.0 %fusion.55 = f32[32,4096]{1,0:T(8,128)S(1)} fusion(bf16[1024,4096]{1,0:T(8,128)(2,1)} %get-tuple-element.171, bf16[32,1024]{1,0:T(8,128)(2,1)S(1)} %get-tuple-element.157, bf16[32]{0:T(256)(128)(2,1)S(1)} %get-tuple-element.142), kind=kOutput, calls=%fused_computation.24.clone.1 | convolution fusion | flops 268468224 | bytes 8978496 | tf_op jit(solution)/shard_map/while/body/eval_jaxpr/dot_general | solution.py:39
  385.0 1.1 constant_dynamic-slice_fusion.3
  387.2 2.0 convolution_convert_fusion
  389.2 2.2 reshape.112
  391.5 3.8 copy.48
  395.2 28.5 %all_to_all.30 = bf16[32,2,16,1024]{3,1,2,0:T(2,128)(2,1)S(1)} all-to-all(bf16[32,2,16,1024]{3,1,2,0:T(2,128)(2,1)S(1)} %copy.48), channel_id=1, replica_groups=mesh['batch'=32,'head'=4] {'head'}, dimensions={0} | all-to-all | bytes 4194304 | tf_op jit(solution)/shard_map/all_to_all | solution.py:93
  424.4 8.3 %maximum_convert_fusion = bf16[8,128,1024]{2,1,0:T(8,128)(2,1)S(1)} fusion(bf16[8,128,1024]{2,1,0:T(8,128)(2,1)S(1)} %bitcast.88, bf16[8,1024,1024]{2,1,0:T(8,128)(2,1)} %param.25), kind=kOutput, calls=%fused_computation.31 | convolution fusion | flops 2149580800 | bytes 20971520 | tf_op jit(solution)/shard_map/prh,phk->prk/dot_general | solution.py:96
  434.7 6.6 %all_to_all.31 = bf16[4,2,2304]{2,1,0:T(2,128)(2,1)S(1)} all-to-all(bf16[4,2,2304]{2,1,0:T(2,128)(2,1)S(1)} %reshape.120), channel_id=1, replica_groups=mesh['batch'=32,'head'=4] {'head'}, dimensions={0} | all-to-all | bytes 73728 | tf_op jit(solution)/shard_map/all_to_all | solution.py:107
  (121 shorter events, 34.8 us)
Async XLA Ops:
  7.2 425.5 %copy-start = (bf16[8,512,18]{1,0,2:T(8,128)(2,1)S(1)}, bf16[8,512,18]{1,0,2:T(8,128)(2,1)}, u32[]{:S(2)}) copy-start(bf16[8,512,18]{1,0,2:T(8,128)(2,1)} %param.27) | copy-start | bytes 442372
  7.2 10.6 %copy-start.1 = (bf16[32,24,512]{2,1,0:T(8,128)(2,1)S(1)}, bf16[32,24,512]{2,1,0:T(8,128)(2,1)}, u32[]{:S(2)}) copy-start(bf16[32,24,512]{2,1,0:T(8,128)(2,1)} %param.15) | copy-start | bytes 2359300
  7.2 10.9 %copy-start.9 = (s32[32]{0:T(128)S(1)}, s32[32]{0:T(128)}, u32[]{:S(2)}) copy-start(s32[32]{0:T(128)} %param.18) | copy-start | bytes 388
  7.2 10.9 %copy-start.7 = (s32[32,1]{0,1:T(1,128)S(1)}, s32[32,1]{0,1:T(1,128)}, u32[]{:S(2)}) copy-start(s32[32,1]{0,1:T(1,128)} %param.20) | copy-start | bytes 388
  7.2 11.1 %copy-start.5 = (s32[32,24]{0,1:T(8,128)S(1)}, s32[32,24]{0,1:T(8,128)}, u32[]{:S(2)}) copy-start(s32[32,24]{0,1:T(8,128)} %param.19) | copy-start | bytes 9220
  7.2 11.1 %copy-start.4 = (bf16[32,1024]{1,0:T(8,128)(2,1)S(1)}, bf16[32,1024]{1,0:T(8,128)(2,1)}, u32[]{:S(2)}) copy-start(bf16[32,1024]{1,0:T(8,128)(2,1)} %param.16) | copy-start | bytes 196612
  7.2 11.1 %copy-start.3 = (bf16[32,1024]{1,0:T(8,128)(2,1)S(1)}, bf16[32,1024]{1,0:T(8,128)(2,1)}, u32[]{:S(2)}) copy-start(bf16[32,1024]{1,0:T(8,128)(2,1)} %param.17) | copy-start | bytes 196612
  7.2 90.3 %all-gather.3.cloned.1.call-start = ((), (), s32[]{:S(2)}) async-start(), calls=%async_computation.2 | async-start | bytes 4325376 | tf_op jit(solution)/shard_map/all_gather | solution.py:73
  16.9 185.2 %all-gather.5.cloned.1.call-start = ((), (), s32[]{:S(2)}) async-start(), calls=%async_computation.3 | async-start | bytes 8650752 | tf_op jit(solution)/shard_map/all_gather | solution.py:77
  202.1 12.1 %copy-start.2 = (f32[4,1024]{1,0:T(4,128)S(1)}, f32[4,1024]{1,0:T(4,128)}, u32[]{:S(2)}) copy-start(f32[4,1024]{1,0:T(4,128)} %param.24) | copy-start | bytes 49156
  424.4 8.7 %copy-start.8 = (bf16[8,512]{1,0:T(8,128)(2,1)S(1)}, bf16[8,512]{1,0:T(8,128)(2,1)}, u32[]{:S(2)}) copy-start(bf16[8,512]{1,0:T(8,128)(2,1)} %param.26) | copy-start | bytes 24580
  433.1 9.2 %copy-start.6 = (s32[32,16]{0,1:T(8,128)S(1)}, s32[32,16]{0,1:T(8,128)}, u32[]{:S(2)}) copy-start(s32[32,16]{0,1:T(8,128)} %param.21) | copy-start | bytes 6148
Sparse Core Ops, SparseCore 0:
  17.0 80.4 all-gather.2
  100.6 101.4 all-gather.4
where the time goes:
time: 454 us; the launch traced here: 451 us
  waiting for transfers between devices  144 us (32%)
  matrix products  138 us (30%)
  local copies, waits for them, and re-layouts  82.2 us (18%)
  blocking collectives  43 us (9%)
  other arithmetic  28.7 us (6%)
  between operations  14.3 us (3%)
    dot_general x24, matrix products, lstm_cell(): jnp.dot(full_h, w_flat, preferred_element_type=jnp.float32)  119 us
    all_gather x1, waiting for transfers between devices, shards(): lax.all_gather(w_in_rows, 'batch', axis=0, tiled=True)  79.2 us
    all_gather x1, waiting for transfers between devices, shards(): lax.all_gather(w_rec_rows, 'batch', axis=0, tiled=True)  65.1 us
    all_to_all x1, blocking collectives, shards(): lax.all_to_all(packed, 'head', split_axis=0, concat_axis=1, tiled=True)  28.5 us
    dynamic_slice x24, local copies, waits for them, and re-layouts, shards(): lax.scan(advance, (start_h, start_c.astype(jnp.float32)), (pre, keeps))  26 us
    dynamic_update_slice x24, other arithmetic, shards(): lax.scan(advance, (start_h, start_c.astype(jnp.float32)), (pre, keeps))  19 us
    unnamed x26, local copies, waits for them, and re-layouts  18.5 us
    reshape x1, local copies, waits for them, and re-layouts, shards(): jnp.dot(feat_flat, w_in_full, preferred_element_type=jnp.float32)  15.6 us
  transfers between devices with their start and end apart: 2, of which 2 were waited for; matrix products, arithmetic and copies ran while one was open for 9% of the time, Pallas kernels for 0%

commit v1 on v0

--- a/solution.py
+++ b/solution.py
@@ -74,7 +74,9 @@
     pre = jnp.dot(feat_flat, w_in_full, preferred_element_type=jnp.float32).reshape(
         steps, seq_dev, 4, width_h
     )
-    w_flat = lax.all_gather(w_rec_rows, "batch", axis=0, tiled=True).reshape(width_h, 4 * width_h)
+    w_flat = jnp.concatenate(
+        lax.all_to_all(jnp.stack([w_rec_rows] * lax.axis_size("batch")), "batch", 0, 0), axis=0
+    ).reshape(width_h, 4 * width_h)
     keeps = 1.0 - ends.astype(jnp.float32).T
 
     def advance(carry, inputs):

time: 454 us -> 480 us (1.057)
  starting transfers between devices: 0.08 us -> 10.7 us
  waiting for transfers between devices: 144 us -> 153 us
  local copies, waits for them, and re-layouts: 82.2 us -> 88.6 us
    all_gather x1, waiting for transfers between devices: 79.2 us -> 153 us  [shards(): lax.all_gather(w_in_rows, 'batch', axis=0, tiled=True)]
    all_gather x1 -> x0, waiting for transfers between devices: 65.1 us -> none  [shards(): lax.all_gather(w_rec_rows, 'batch', axis=0, tiled=True)]
    all_to_all x0 -> x1, starting transfers between devices: none -> 10.7 us  [shards(): lax.all_to_all(jnp.stack([w_rec_rows] * lax.axis_size('batch')), 'batch',...]
    another operation x0 -> x1, local copies, waits for them, and re-layouts: none -> 7.12 us  [shards(): jnp.stack([w_rec_rows] * lax.axis_size('batch'))]
  transfers between devices with their start and end apart: 2 -> 2, of which waited for: 2 -> 1; matrix products, arithmetic and copies ran while one was open for 9% -> 10% of each run, Pallas kernels for 0% -> 0%
where the time goes in v1:
time: 480 us; the launch traced here: 477 us
  waiting for transfers between devices  153 us (32%)
  matrix products  138 us (29%)
  local copies, waits for them, and re-layouts  88.6 us (18%)
  blocking collectives  43 us (9%)
  other arithmetic  28.8 us (6%)
  between operations  14.3 us (3%)
  starting transfers between devices  10.7 us (2%)
    all_gather x1, waiting for transfers between devices, shards(): lax.all_gather(w_in_rows, 'batch', axis=0, tiled=True)  153 us
    dot_general x24, matrix products, lstm_cell(): jnp.dot(full_h, w_flat, preferred_element_type=jnp.float32)  119 us
    all_to_all x1, blocking collectives, shards(): lax.all_to_all(packed, 'head', split_axis=0, concat_axis=1, tiled=True)  28.5 us
    dynamic_slice x24, local copies, waits for them, and re-layouts, shards(): lax.scan(advance, (start_h, start_c.astype(jnp.float32)), (pre, keeps))  26 us
    dynamic_update_slice x24, other arithmetic, shards(): lax.scan(advance, (start_h, start_c.astype(jnp.float32)), (pre, keeps))  19.1 us
    unnamed x26, local copies, waits for them, and re-layouts  18.5 us
    reshape x1, local copies, waits for them, and re-layouts, shards(): jnp.dot(feat_flat, w_in_full, preferred_element_type=jnp.float32)  15.6 us
    dot_general x1, local copies, waits for them, and re-layouts, shards(): jnp.dot(feat_flat, w_in_full, preferred_element_type=jnp.float32)  12.7 us
  transfers between devices with their start and end apart: 2, of which 1 were waited for; matrix products, arithmetic and copies ran while one was open for 10% of the time, Pallas kernels for 0%

profile of v1, /device:TPU:1, one launch (start us, length us, event | category | flops | bytes accessed | tf_op | source)
XLA Modules:
  0.0 476.6 jit_solution(2480667240800114405)
XLA Ops:
  8.2 7.9 %all_gather.6 = bf16[48,4,1024]{2,1,0:T(4,128)(2,1)S(1)} all-gather(bf16[48,4,256]{2,1,0:T(4,128)(2,1)S(1)} %pad_maximum_fusion), channel_id=1, replica_groups=mesh['batch'=32,'head'=4] {'head'}, dimensions={2}, use_global_device_ids=true | all-gather | bytes 491520 | tf_op jit(solution)/shard_map/all_gather | solution.py:14
  16.9 7.1 %stack.2 = bf16[32,32,4,1024]{3,2,1,0:T(4,128)(2,1)} broadcast(bf16[32,4,1024]{2,1,0:T(4,128)(2,1)S(1)} %split.9), dimensions={1,2,3} | broadcast | bytes 8650752 | tf_op jit(solution)/shard_map/stack | solution.py:78
  24.1 10.7 %all-to-all-start = ((bf16[32,32,4,1024]{3,2,1,0:T(4,128)(2,1)}), bf16[32,32,4,1024]{3,2,1,0:T(4,128)(2,1)}, u32[]{:S(2)}, u32[]{:S(2)}) async-start(bf16[32,32,4,1024]{3,2,1,0:T(4,128)(2,1)} %stack.2), calls=%async_computation | async-start | bytes 16777216 | tf_op jit(solution)/shard_map/all_to_all | solution.py:78
  35.4 153.2 %all-gather.2.cloned.1.call-done = bf16[512,4,1024]{2,1,0:T(4,128)(2,1)} async-done(((bf16[16,4,1024]{2,1,0:T(4,128)(2,1)}), bf16[512,4,1024]{2,1,0:T(4,128)(2,1)}) %all-gather.2.cloned.1.call-update) | async-done | bytes 4194320 | tf_op jit(solution)/shard_map/all_gather | solution.py:73
  188.6 4.5 copy.61
  193.1 6.4 %convolution_bitcast_fusion = f32[768,4096]{0,1:T(8,128)} fusion(bf16[512,4096]{1,0:T(8,128)(2,1)S(1)} %bitcast.92, bf16[768,512]{1,0:T(8,128)(2,1)S(1)} %bitcast.96), kind=kOutput, calls=%fused_computation.30 | convolution fusion | flops 3221225472 | bytes 17563648 | tf_op jit(solution)/shard_map/dot_general | solution.py:74
  199.5 12.7 %copy.47 = f32[768,4096]{1,0:T(8,128)} copy(f32[768,4096]{0,1:T(8,128)} %convolution_bitcast_fusion) | data formatting | bytes 25165824 | tf_op jit(solution)/shard_map/dot_general | solution.py:74
  212.2 15.6 %reshape.109 = f32[24,32,4,1024]{3,2,1,0:T(4,128)} reshape(f32[768,4096]{1,0:T(8,128)} %copy.47) | data formatting | bytes 25165824 | tf_op jit(solution)/shard_map/reshape | solution.py:74
  227.8 12.1 %copy.62 = bf16[128,8,4,1024]{3,1,2,0:T(8,128)(2,1)} copy(bf16[128,8,4,1024]{3,2,1,0:T(4,128)(2,1)} %bitcast.28) | data formatting | bytes 16777216
  239.9 173.2 %while.14 = (s32[]{:T(128)}, bf16[32,1024]{1,0:T(8,128)(2,1)S(1)}, f32[32,1024]{1,0:T(8,128)S(1)}, bf16[24,32,1024]{2,1,0:T(8,128)(2,1)}, f32[24,32,4,1024]{3,2,...) while((s32[]{:T(128)}, bf16[32,1024]{1,0:T(8,128)(2,1)S(1)}, ...), condition=%wide.region_2.3_spmd, body=%wide.region_1.2_spmd.sunk | while | flops 269221920 | bytes 12534885 | solution.py:88
  239.9 5.0 %fusion.55 = f32[32,4096]{1,0:T(8,128)S(1)} fusion(bf16[1024,4096]{1,0:T(8,128)(2,1)} %get-tuple-element.171, bf16[32,1024]{1,0:T(8,128)(2,1)S(1)} %get-tuple-element.157, bf16[32]{0:T(256)(128)(2,1)S(1)} %get-tuple-element.142), kind=kOutput, calls=%fused_computation.24.clone.1 | convolution fusion | flops 268468224 | bytes 8978496 | tf_op jit(solution)/shard_map/while/body/eval_jaxpr/dot_general | solution.py:39
  244.9 1.1 constant_dynamic-slice_fusion.3
  247.1 5.0 %fusion.55 = f32[32,4096]{1,0:T(8,128)S(1)} fusion(bf16[1024,4096]{1,0:T(8,128)(2,1)} %get-tuple-element.171, bf16[32,1024]{1,0:T(8,128)(2,1)S(1)} %get-tuple-element.157, bf16[32]{0:T(256)(128)(2,1)S(1)} %get-tuple-element.142), kind=kOutput, calls=%fused_computation.24.clone.1 | convolution fusion | flops 268468224 | bytes 8978496 | tf_op jit(solution)/shard_map/while/body/eval_jaxpr/dot_general | solution.py:39
  252.1 1.1 constant_dynamic-slice_fusion.3
  254.4 5.0 %fusion.55 = f32[32,4096]{1,0:T(8,128)S(1)} fusion(bf16[1024,4096]{1,0:T(8,128)(2,1)} %get-tuple-element.171, bf16[32,1024]{1,0:T(8,128)(2,1)S(1)} %get-tuple-element.157, bf16[32]{0:T(256)(128)(2,1)S(1)} %get-tuple-element.142), kind=kOutput, calls=%fused_computation.24.clone.1 | convolution fusion | flops 268468224 | bytes 8978496 | tf_op jit(solution)/shard_map/while/body/eval_jaxpr/dot_general | solution.py:39
  259.3 1.1 constant_dynamic-slice_fusion.3
  261.6 5.0 %fusion.55 = f32[32,4096]{1,0:T(8,128)S(1)} fusion(bf16[1024,4096]{1,0:T(8,128)(2,1)} %get-tuple-element.171, bf16[32,1024]{1,0:T(8,128)(2,1)S(1)} %get-tuple-element.157, bf16[32]{0:T(256)(128)(2,1)S(1)} %get-tuple-element.142), kind=kOutput, calls=%fused_computation.24.clone.1 | convolution fusion | flops 268468224 | bytes 8978496 | tf_op jit(solution)/shard_map/while/body/eval_jaxpr/dot_general | solution.py:39
  266.6 1.1 constant_dynamic-slice_fusion.3
  268.8 5.0 %fusion.55 = f32[32,4096]{1,0:T(8,128)S(1)} fusion(bf16[1024,4096]{1,0:T(8,128)(2,1)} %get-tuple-element.171, bf16[32,1024]{1,0:T(8,128)(2,1)S(1)} %get-tuple-element.157, bf16[32]{0:T(256)(128)(2,1)S(1)} %get-tuple-element.142), kind=kOutput, calls=%fused_computation.24.clone.1 | convolution fusion | flops 268468224 | bytes 8978496 | tf_op jit(solution)/shard_map/while/body/eval_jaxpr/dot_general | solution.py:39
  273.8 1.1 constant_dynamic-slice_fusion.3
  276.0 5.0 %fusion.55 = f32[32,4096]{1,0:T(8,128)S(1)} fusion(bf16[1024,4096]{1,0:T(8,128)(2,1)} %get-tuple-element.171, bf16[32,1024]{1,0:T(8,128)(2,1)S(1)} %get-tuple-element.157, bf16[32]{0:T(256)(128)(2,1)S(1)} %get-tuple-element.142), kind=kOutput, calls=%fused_computation.24.clone.1 | convolution fusion | flops 268468224 | bytes 8978496 | tf_op jit(solution)/shard_map/while/body/eval_jaxpr/dot_general | solution.py:39
  281.0 1.1 constant_dynamic-slice_fusion.3
  283.2 5.0 %fusion.55 = f32[32,4096]{1,0:T(8,128)S(1)} fusion(bf16[1024,4096]{1,0:T(8,128)(2,1)} %get-tuple-element.171, bf16[32,1024]{1,0:T(8,128)(2,1)S(1)} %get-tuple-element.157, bf16[32]{0:T(256)(128)(2,1)S(1)} %get-tuple-element.142), kind=kOutput, calls=%fused_computation.24.clone.1 | convolution fusion | flops 268468224 | bytes 8978496 | tf_op jit(solution)/shard_map/while/body/eval_jaxpr/dot_general | solution.py:39
  288.2 1.1 constant_dynamic-slice_fusion.3
  290.4 5.0 %fusion.55 = f32[32,4096]{1,0:T(8,128)S(1)} fusion(bf16[1024,4096]{1,0:T(8,128)(2,1)} %get-tuple-element.171, bf16[32,1024]{1,0:T(8,128)(2,1)S(1)} %get-tuple-element.157, bf16[32]{0:T(256)(128)(2,1)S(1)} %get-tuple-element.142), kind=kOutput, calls=%fused_computation.24.clone.1 | convolution fusion | flops 268468224 | bytes 8978496 | tf_op jit(solution)/shard_map/while/body/eval_jaxpr/dot_general | solution.py:39
  295.4 1.1 constant_dynamic-slice_fusion.3
  297.6 5.0 %fusion.55 = f32[32,4096]{1,0:T(8,128)S(1)} fusion(bf16[1024,4096]{1,0:T(8,128)(2,1)} %get-tuple-element.171, bf16[32,1024]{1,0:T(8,128)(2,1)S(1)} %get-tuple-element.157, bf16[32]{0:T(256)(128)(2,1)S(1)} %get-tuple-element.142), kind=kOutput, calls=%fused_computation.24.clone.1 | convolution fusion | flops 268468224 | bytes 8978496 | tf_op jit(solution)/shard_map/while/body/eval_jaxpr/dot_general | solution.py:39
  302.6 1.1 constant_dynamic-slice_fusion.3
  304.8 5.0 %fusion.55 = f32[32,4096]{1,0:T(8,128)S(1)} fusion(bf16[1024,4096]{1,0:T(8,128)(2,1)} %get-tuple-element.171, bf16[32,1024]{1,0:T(8,128)(2,1)S(1)} %get-tuple-element.157, bf16[32]{0:T(256)(128)(2,1)S(1)} %get-tuple-element.142), kind=kOutput, calls=%fused_computation.24.clone.1 | convolution fusion | flops 268468224 | bytes 8978496 | tf_op jit(solution)/shard_map/while/body/eval_jaxpr/dot_general | solution.py:39
  309.8 1.1 constant_dynamic-slice_fusion.3
  312.1 5.0 %fusion.55 = f32[32,4096]{1,0:T(8,128)S(1)} fusion(bf16[1024,4096]{1,0:T(8,128)(2,1)} %get-tuple-element.171, bf16[32,1024]{1,0:T(8,128)(2,1)S(1)} %get-tuple-element.157, bf16[32]{0:T(256)(128)(2,1)S(1)} %get-tuple-element.142), kind=kOutput, calls=%fused_computation.24.clone.1 | convolution fusion | flops 268468224 | bytes 8978496 | tf_op jit(solution)/shard_map/while/body/eval_jaxpr/dot_general | solution.py:39
  317.1 1.1 constant_dynamic-slice_fusion.3
  319.3 5.0 %fusion.55 = f32[32,4096]{1,0:T(8,128)S(1)} fusion(bf16[1024,4096]{1,0:T(8,128)(2,1)} %get-tuple-element.171, bf16[32,1024]{1,0:T(8,128)(2,1)S(1)} %get-tuple-element.157, bf16[32]{0:T(256)(128)(2,1)S(1)} %get-tuple-element.142), kind=kOutput, calls=%fused_computation.24.clone.1 | convolution fusion | flops 268468224 | bytes 8978496 | tf_op jit(solution)/shard_map/while/body/eval_jaxpr/dot_general | solution.py:39
  324.3 1.1 constant_dynamic-slice_fusion.3
  326.5 5.0 %fusion.55 = f32[32,4096]{1,0:T(8,128)S(1)} fusion(bf16[1024,4096]{1,0:T(8,128)(2,1)} %get-tuple-element.171, bf16[32,1024]{1,0:T(8,128)(2,1)S(1)} %get-tuple-element.157, bf16[32]{0:T(256)(128)(2,1)S(1)} %get-tuple-element.142), kind=kOutput, calls=%fused_computation.24.clone.1 | convolution fusion | flops 268468224 | bytes 8978496 | tf_op jit(solution)/shard_map/while/body/eval_jaxpr/dot_general | solution.py:39
  331.5 1.1 constant_dynamic-slice_fusion.3
  333.7 5.0 %fusion.55 = f32[32,4096]{1,0:T(8,128)S(1)} fusion(bf16[1024,4096]{1,0:T(8,128)(2,1)} %get-tuple-element.171, bf16[32,1024]{1,0:T(8,128)(2,1)S(1)} %get-tuple-element.157, bf16[32]{0:T(256)(128)(2,1)S(1)} %get-tuple-element.142), kind=kOutput, calls=%fused_computation.24.clone.1 | convolution fusion | flops 268468224 | bytes 8978496 | tf_op jit(solution)/shard_map/while/body/eval_jaxpr/dot_general | solution.py:39
  338.7 1.1 constant_dynamic-slice_fusion.3
  341.0 5.0 %fusion.55 = f32[32,4096]{1,0:T(8,128)S(1)} fusion(bf16[1024,4096]{1,0:T(8,128)(2,1)} %get-tuple-element.171, bf16[32,1024]{1,0:T(8,128)(2,1)S(1)} %get-tuple-element.157, bf16[32]{0:T(256)(128)(2,1)S(1)} %get-tuple-element.142), kind=kOutput, calls=%fused_computation.24.clone.1 | convolution fusion | flops 268468224 | bytes 8978496 | tf_op jit(solution)/shard_map/while/body/eval_jaxpr/dot_general | solution.py:39
  345.9 1.1 constant_dynamic-slice_fusion.3
  348.2 5.0 %fusion.55 = f32[32,4096]{1,0:T(8,128)S(1)} fusion(bf16[1024,4096]{1,0:T(8,128)(2,1)} %get-tuple-element.171, bf16[32,1024]{1,0:T(8,128)(2,1)S(1)} %get-tuple-element.157, bf16[32]{0:T(256)(128)(2,1)S(1)} %get-tuple-element.142), kind=kOutput, calls=%fused_computation.24.clone.1 | convolution fusion | flops 268468224 | bytes 8978496 | tf_op jit(solution)/shard_map/while/body/eval_jaxpr/dot_general | solution.py:39
  353.1 1.1 constant_dynamic-slice_fusion.3
  355.4 5.0 %fusion.55 = f32[32,4096]{1,0:T(8,128)S(1)} fusion(bf16[1024,4096]{1,0:T(8,128)(2,1)} %get-tuple-element.171, bf16[32,1024]{1,0:T(8,128)(2,1)S(1)} %get-tuple-element.157, bf16[32]{0:T(256)(128)(2,1)S(1)} %get-tuple-element.142), kind=kOutput, calls=%fused_computation.24.clone.1 | convolution fusion | flops 268468224 | bytes 8978496 | tf_op jit(solution)/shard_map/while/body/eval_jaxpr/dot_general | solution.py:39
  360.4 1.1 constant_dynamic-slice_fusion.3
  362.6 5.0 %fusion.55 = f32[32,4096]{1,0:T(8,128)S(1)} fusion(bf16[1024,4096]{1,0:T(8,128)(2,1)} %get-tuple-element.171, bf16[32,1024]{1,0:T(8,128)(2,1)S(1)} %get-tuple-element.157, bf16[32]{0:T(256)(128)(2,1)S(1)} %get-tuple-element.142), kind=kOutput, calls=%fused_computation.24.clone.1 | convolution fusion | flops 268468224 | bytes 8978496 | tf_op jit(solution)/shard_map/while/body/eval_jaxpr/dot_general | solution.py:39
  367.6 1.1 constant_dynamic-slice_fusion.3
  369.8 5.0 %fusion.55 = f32[32,4096]{1,0:T(8,128)S(1)} fusion(bf16[1024,4096]{1,0:T(8,128)(2,1)} %get-tuple-element.171, bf16[32,1024]{1,0:T(8,128)(2,1)S(1)} %get-tuple-element.157, bf16[32]{0:T(256)(128)(2,1)S(1)} %get-tuple-element.142), kind=kOutput, calls=%fused_computation.24.clone.1 | convolution fusion | flops 268468224 | bytes 8978496 | tf_op jit(solution)/shard_map/while/body/eval_jaxpr/dot_general | solution.py:39
  374.8 1.1 constant_dynamic-slice_fusion.3
  377.0 5.0 %fusion.55 = f32[32,4096]{1,0:T(8,128)S(1)} fusion(bf16[1024,4096]{1,0:T(8,128)(2,1)} %get-tuple-element.171, bf16[32,1024]{1,0:T(8,128)(2,1)S(1)} %get-tuple-element.157, bf16[32]{0:T(256)(128)(2,1)S(1)} %get-tuple-element.142), kind=kOutput, calls=%fused_computation.24.clone.1 | convolution fusion | flops 268468224 | bytes 8978496 | tf_op jit(solution)/shard_map/while/body/eval_jaxpr/dot_general | solution.py:39
  382.0 1.1 constant_dynamic-slice_fusion.3
  384.2 5.0 %fusion.55 = f32[32,4096]{1,0:T(8,128)S(1)} fusion(bf16[1024,4096]{1,0:T(8,128)(2,1)} %get-tuple-element.171, bf16[32,1024]{1,0:T(8,128)(2,1)S(1)} %get-tuple-element.157, bf16[32]{0:T(256)(128)(2,1)S(1)} %get-tuple-element.142), kind=kOutput, calls=%fused_computation.24.clone.1 | convolution fusion | flops 268468224 | bytes 8978496 | tf_op jit(solution)/shard_map/while/body/eval_jaxpr/dot_general | solution.py:39
  389.2 1.1 constant_dynamic-slice_fusion.3
  391.5 5.0 %fusion.55 = f32[32,4096]{1,0:T(8,128)S(1)} fusion(bf16[1024,4096]{1,0:T(8,128)(2,1)} %get-tuple-element.171, bf16[32,1024]{1,0:T(8,128)(2,1)S(1)} %get-tuple-element.157, bf16[32]{0:T(256)(128)(2,1)S(1)} %get-tuple-element.142), kind=kOutput, calls=%fused_computation.24.clone.1 | convolution fusion | flops 268468224 | bytes 8978496 | tf_op jit(solution)/shard_map/while/body/eval_jaxpr/dot_general | solution.py:39
  396.4 1.1 constant_dynamic-slice_fusion.3
  398.7 5.0 %fusion.55 = f32[32,4096]{1,0:T(8,128)S(1)} fusion(bf16[1024,4096]{1,0:T(8,128)(2,1)} %get-tuple-element.171, bf16[32,1024]{1,0:T(8,128)(2,1)S(1)} %get-tuple-element.157, bf16[32]{0:T(256)(128)(2,1)S(1)} %get-tuple-element.142), kind=kOutput, calls=%fused_computation.24.clone.1 | convolution fusion | flops 268468224 | bytes 8978496 | tf_op jit(solution)/shard_map/while/body/eval_jaxpr/dot_general | solution.py:39
  403.6 1.1 constant_dynamic-slice_fusion.3
  405.9 5.0 %fusion.55 = f32[32,4096]{1,0:T(8,128)S(1)} fusion(bf16[1024,4096]{1,0:T(8,128)(2,1)} %get-tuple-element.171, bf16[32,1024]{1,0:T(8,128)(2,1)S(1)} %get-tuple-element.157, bf16[32]{0:T(256)(128)(2,1)S(1)} %get-tuple-element.142), kind=kOutput, calls=%fused_computation.24.clone.1 | convolution fusion | flops 268468224 | bytes 8978496 | tf_op jit(solution)/shard_map/while/body/eval_jaxpr/dot_general | solution.py:39
  410.8 1.1 constant_dynamic-slice_fusion.3
  413.1 2.0 convolution_convert_fusion
  415.1 2.2 reshape.110
  417.4 3.8 copy.48
  421.1 28.5 %all_to_all.35 = bf16[32,2,16,1024]{3,1,2,0:T(2,128)(2,1)S(1)} all-to-all(bf16[32,2,16,1024]{3,1,2,0:T(2,128)(2,1)S(1)} %copy.48), channel_id=1, replica_groups=mesh['batch'=32,'head'=4] {'head'}, dimensions={0} | all-to-all | bytes 4194304 | tf_op jit(solution)/shard_map/all_to_all | solution.py:95
  450.3 8.3 %maximum_convert_fusion = bf16[8,128,1024]{2,1,0:T(8,128)(2,1)S(1)} fusion(bf16[8,128,1024]{2,1,0:T(8,128)(2,1)S(1)} %bitcast.89, bf16[8,1024,1024]{2,1,0:T(8,128)(2,1)} %param.25), kind=kOutput, calls=%fused_computation.31 | convolution fusion | flops 2149580800 | bytes 20971520 | tf_op jit(solution)/shard_map/prh,phk->prk/dot_general | solution.py:98
  460.6 6.6 %all_to_all.36 = bf16[4,2,2304]{2,1,0:T(2,128)(2,1)S(1)} all-to-all(bf16[4,2,2304]{2,1,0:T(2,128)(2,1)S(1)} %reshape.118), channel_id=1, replica_groups=mesh['batch'=32,'head'=4] {'head'}, dimensions={0} | all-to-all | bytes 73728 | tf_op jit(solution)/shard_map/all_to_all | solution.py:109
  (121 shorter events, 35.1 us)
Async XLA Ops:
  7.2 451.4 %copy-start = (bf16[8,512,18]{1,0,2:T(8,128)(2,1)S(1)}, bf16[8,512,18]{1,0,2:T(8,128)(2,1)}, u32[]{:S(2)}) copy-start(bf16[8,512,18]{1,0,2:T(8,128)(2,1)} %param.27) | copy-start | bytes 442372
  7.2 181.4 %all-gather.2.cloned.1.call-start = ((), (), s32[]{:S(2)}) async-start(), calls=%async_computation.3 | async-start | bytes 4325376 | tf_op jit(solution)/shard_map/all_gather | solution.py:73
  24.0 10.8 %copy-start.1 = (bf16[32,24,512]{2,1,0:T(8,128)(2,1)S(1)}, bf16[32,24,512]{2,1,0:T(8,128)(2,1)}, u32[]{:S(2)}) copy-start(bf16[32,24,512]{2,1,0:T(8,128)(2,1)} %param.15) | copy-start | bytes 2359300
  24.0 11.0 %copy-start.9 = (s32[32]{0:T(128)S(1)}, s32[32]{0:T(128)}, u32[]{:S(2)}) copy-start(s32[32]{0:T(128)} %param.18) | copy-start | bytes 388
  24.0 11.0 %copy-start.7 = (s32[32,1]{0,1:T(1,128)S(1)}, s32[32,1]{0,1:T(1,128)}, u32[]{:S(2)}) copy-start(s32[32,1]{0,1:T(1,128)} %param.20) | copy-start | bytes 388
  24.0 11.2 %copy-start.5 = (s32[32,24]{0,1:T(8,128)S(1)}, s32[32,24]{0,1:T(8,128)}, u32[]{:S(2)}) copy-start(s32[32,24]{0,1:T(8,128)} %param.19) | copy-start | bytes 9220
  24.0 11.2 %copy-start.3 = (bf16[32,1024]{1,0:T(8,128)(2,1)S(1)}, bf16[32,1024]{1,0:T(8,128)(2,1)}, u32[]{:S(2)}) copy-start(bf16[32,1024]{1,0:T(8,128)(2,1)} %param.17) | copy-start | bytes 196612
  24.1 11.2 %copy-start.4 = (bf16[32,1024]{1,0:T(8,128)(2,1)S(1)}, bf16[32,1024]{1,0:T(8,128)(2,1)}, u32[]{:S(2)}) copy-start(bf16[32,1024]{1,0:T(8,128)(2,1)} %param.16) | copy-start | bytes 196612
  24.1 203.7 %all-to-all-start = ((bf16[32,32,4,1024]{3,2,1,0:T(4,128)(2,1)}), bf16[32,32,4,1024]{3,2,1,0:T(4,128)(2,1)}, u32[]{:S(2)}, u32[]{:S(2)}) async-start(bf16[32,32,4,1024]{3,2,1,0:T(4,128)(2,1)} %stack.2), calls=%async_computation | async-start | bytes 16777216 | tf_op jit(solution)/shard_map/all_to_all | solution.py:78
  227.8 12.1 %copy-start.2 = (f32[4,1024]{1,0:T(4,128)S(1)}, f32[4,1024]{1,0:T(4,128)}, u32[]{:S(2)}) copy-start(f32[4,1024]{1,0:T(4,128)} %param.24) | copy-start | bytes 49156
  450.3 8.7 %copy-start.8 = (bf16[8,512]{1,0:T(8,128)(2,1)S(1)}, bf16[8,512]{1,0:T(8,128)(2,1)}, u32[]{:S(2)}) copy-start(bf16[8,512]{1,0:T(8,128)(2,1)} %param.26) | copy-start | bytes 24580
  458.6 9.6 %copy-start.6 = (s32[32,16]{0,1:T(8,128)S(1)}, s32[32,16]{0,1:T(8,128)}, u32[]{:S(2)}) copy-start(s32[32,16]{0,1:T(8,128)} %param.21) | copy-start | bytes 6148
Sparse Core Ops, SparseCore 0:
  16.9 171.6 all-gather.1
